TPU v7x, 128 devices: a whole 4x4x4 slice. The times are simulated.
128 devices in a mesh: fit: 8 (over z, core), pair: 16 (over x, y).
Axes of the slice: x: 4, y: 4, z: 4, core: 2. Of those that a mesh axis runs over, the one named last changes fastest.
Arguments:
- metric_factor: bfloat16 [4096, 4096], P('fit'), as said below
- three_index: bfloat16 [4096, 32768], P('fit', 'pair'), may hold values from -6 to 6
- send_map: int32 [16, 16, 8], P('pair'), may hold values from 0 to 15
- pair_slots: int32 [16, 128], P('pair'), may hold values from 0 to 127, each once within a row
- pair_count: int32 [16], P('pair'), may hold values from 1 to 64, 512 in all
- orbital_energy: bfloat16 [256], P('pair'), may hold values from -2 to -0.19921875
- cabs_energy: float32 [1024], replicated, may hold values from 0.5 to 4
- coupling: bfloat16 [128, 1024], replicated, may hold values from -0.5 to 0.5
Outputs:
- projected: bfloat16 [16, 64, 128, 1024], P('pair', 'fit')
Inputs may be any that keep to these rules, and one draw needn't show every extreme that they name: `metric_factor`: diagonal entries lie between 0.6 and 1.4. `pair_slots`: each row holds every position 0 to 127 once; pair n of a row uses entries 2n and 2n + 1.
All inputs are finite; a program needn't handle non-finite values. No bound on the sum of `pair_count` on one device may be relied on, other than what follows from the above.
Results may differ from a plain program's by a relative error of at most 0.015.
Values may be sent and summed in bfloat16 or wider, within the bound.
A program may use at most 256 MiB of HBM per device.

v0:
```python
import jax
import jax.numpy as jnp
from jax import lax
from jax.sharding import PartitionSpec as P

NAUX = 4096
PAIR_BLOCK = 8


def turned_gather(arrays, axis, dims):
    turned = [jnp.moveaxis(a, dim, 0) for a, dim in zip(arrays, dims)]
    both = jnp.concatenate([t.reshape(len(t), -1) for t in turned], axis=1)
    filled, at, outs = (lax.all_gather(both, axis, axis=0, tiled=True), 0, [])
    for t, dim in zip(turned, dims):
        slab = filled[:, at : at + t[0].size].reshape(-1, *t.shape[1:])
        outs.append(jnp.moveaxis(slab, 0, dim))
        at += t[0].size
    return tuple(outs)


def on_device(
    metric_factor,
    three_index,
    send_map,
    pair_slots,
    pair_count,
    orbital_energy,
    cabs_energy,
    coupling,
):
    domain = coupling.shape[0]
    orbitals = orbital_energy.shape[0]
    local_rows = metric_factor.shape[0]
    peers = send_map.shape[1]
    capacity = send_map.shape[2]
    slot_total = pair_slots.shape[1] // 2
    fitted = jnp.dot(
        metric_factor,
        lax.all_gather(three_index, "fit", axis=0, tiled=True),
        preferred_element_type=jnp.float32,
    )
    fitted = fitted.astype(jnp.bfloat16).reshape(local_rows, orbitals, domain)
    requests = send_map.reshape(peers, capacity)
    source, energy_src = turned_gather((fitted, orbital_energy), "pair", (1, 0))
    global_ids = (jnp.arange(peers, dtype=jnp.int32)[:, None] * orbitals + requests).reshape(-1)
    pair_index = jnp.take(global_ids, pair_slots[0])
    left_index = pair_index[0::2]
    right_index = pair_index[1::2]
    live_count = pair_count[0]
    norm_scale = NAUX ** (-0.5)
    block_count = (live_count + PAIR_BLOCK - 1) // PAIR_BLOCK

    def advance(block, partial_value):
        left_ids = lax.dynamic_slice_in_dim(left_index, block * PAIR_BLOCK, PAIR_BLOCK)
        right_ids = lax.dynamic_slice_in_dim(right_index, block * PAIR_BLOCK, PAIR_BLOCK)
        left_rows = jnp.take(source, left_ids, axis=1)
        right_rows = jnp.take(source, right_ids, axis=1)
        product = jnp.einsum(
            "qsa,qsb->sab", left_rows, right_rows, preferred_element_type=jnp.float32
        )
        return lax.dynamic_update_slice_in_dim(
            partial_value, product * norm_scale, block * PAIR_BLOCK, 0
        )

    partial_value = jnp.zeros((slot_total, domain, domain), jnp.float32)
    partial_value = lax.fori_loop(0, block_count, advance, partial_value)
    share = slot_total // lax.axis_size("fit")
    first_slot = lax.axis_index("fit") * share
    exchange = lax.psum_scatter(
        partial_value.astype(jnp.bfloat16), "fit", scatter_dimension=0, tiled=True
    )
    energy_sum = jnp.take(energy_src, left_index).astype(jnp.float32) + jnp.take(
        energy_src, right_index
    ).astype(jnp.float32)
    energy_sum = lax.dynamic_slice_in_dim(energy_sum, first_slot, share, 0)
    weighted = jnp.einsum("sab,bc->sac", exchange, coupling, preferred_element_type=jnp.float32)
    denom = cabs_energy[None, None, :] - energy_sum[:, None, None]
    live_mask = first_slot + jnp.arange(share, dtype=jnp.int32) < live_count
    projected = jnp.where(live_mask[:, None, None], weighted / denom, 0.0).astype(jnp.bfloat16)
    return projected.reshape(1, share, domain, weighted.shape[2])


def solution(mesh):
    in_specs = (
        P("fit", None),
        P("fit", "pair"),
        P("pair", None, None),
        P("pair", None),
        P("pair"),
        P("pair"),
        P(),
        P(),
    )
    out_specs = P("pair", "fit", None, None)
    return jax.shard_map(
        on_device, mesh=mesh, in_specs=in_specs, out_specs=out_specs, check_vma=False
    )
```

profile of v0, /device:TPU:0, one launch (start us, length us, event | category | flops | bytes accessed | tf_op | source)
XLA Modules:
  0.0 506.7 jit_solution(18273993454955358155)
XLA Ops:
  8.1 88.6 %all-gather.3.cloned.1.call-done = bf16[4096,2048]{1,0:T(8,128)(2,1)} async-done(((bf16[512,2048]{1,0:T(8,128)(2,1)}), bf16[4096,2048]{1,0:T(8,128)(2,1)}) %all-gather.3.cloned.1.call-update) | async-done | bytes 16777232 | tf_op jit(solution)/shard_map/all_gather | solution.py:39
  96.7 13.6 %fusion.9 = bf16[64,16,8,128]{3,2,1,0:T(8,128)(2,1)S(1)} fusion(bf16[512,4096]{1,0:T(8,128)(2,1)} %param.14, bf16[4096,2048]{1,0:T(8,128)(2,1)} %all-gather.3.cloned.1.call-done), kind=kOutput, calls=%fused_computation.26 | convolution fusion | flops 8590983168 | bytes 23068672 | tf_op jit(solution)/shard_map/dot_general | solution.py:37
  116.4 195.1 %all-gather.5.cloned.1.call-done = bf16[256,65537]{1,0:T(8,128)(2,1)} async-done(((bf16[16,65537]{1,0:T(8,128)(2,1)}), bf16[256,65537]{1,0:T(8,128)(2,1)}) %all-gather.5.cloned.1.call-update) | async-done | bytes 33554960 | tf_op jit(solution)/shard_map/all_gather | solution.py:13
  311.5 22.9 %slice.26 = bf16[256,65536]{1,0:T(8,128)(2,1)} slice(bf16[256,65537]{1,0:T(8,128)(2,1)} %all-gather.5.cloned.1.call-done), slice={[0:256], [0:65536]} | slice | bytes 67108864 | tf_op jit(solution)/shard_map/slice | solution.py:15
  334.3 41.6 %copy.17 = bf16[256,65536]{0,1:T(8,128)(2,1)} copy(bf16[256,65536]{1,0:T(8,128)(2,1)} %slice.26) | data formatting | bytes 67108864 | tf_op jit(solution)/shard_map/slice | solution.py:15
  375.9 43.8 %copy.18 = bf16[512,256,128]{2,0,1:T(8,128)(2,1)} copy(bf16[512,256,128]{1,2,0:T(8,128)(2,1)} %bitcast.41) | data formatting | bytes 67108864 | tf_op jit(solution)/shard_map/while | solution.py:66
  421.5 42.6 %while.10 = (s32[]{:T(128)}, bf16[64,128,128]{2,1,0:T(8,128)(2,1)}, s32[]{:T(128)}, s32[64]{0:T(128)S(1)}, bf16[512,256,128]{2,0,1:T(8,128)(2,1)}, /*index=5*/s3...) while((s32[]{:T(128)}, bf16[64,128,128]{2,1,0:T(8,128)(2,1)}, s32[]{:T(128)}, s32[64]{0:T(128)S(1)}, ...), condition=%wide.region_1.3_spmd, body=%wide.region_0.0_spmd.sunk | while | flops 135399520 | bytes 6824379 | solution.py:66
  421.6 2.0 gather_fusion.1
  423.6 2.0 gather_fusion
  426.9 2.0 gather_fusion.1
  428.9 2.0 gather_fusion
  432.2 2.0 gather_fusion.1
  434.2 2.0 gather_fusion
  437.6 2.0 gather_fusion.1
  439.5 2.0 gather_fusion
  442.9 2.0 gather_fusion.1
  444.9 2.0 gather_fusion
  448.2 2.0 gather_fusion.1
  450.2 2.0 gather_fusion
  453.5 2.0 gather_fusion.1
  455.5 2.0 gather_fusion
  458.9 2.0 gather_fusion.1
  466.8 30.3 %reduce-scatter.2.cloned.1.call-done = bf16[8,128,128]{2,1,0:T(8,128)(2,1)} async-done(((bf16[64,128,128]{2,1,0:T(8,128)(2,1)}), bf16[8,128,128]{2,1,0:T(8,128)(2,1)}) %reduce-scatter.2.cloned.1.call-update) | async-done | bytes 262160 | tf_op jit(solution)/shard_map/reduce_scatter | solution.py:69
  497.2 3.0 fusion.10
  (75 shorter events, 24.4 us)
Async XLA Ops:
  6.5 490.6 %copy-start = (bf16[128,1024]{1,0:T(8,128)(2,1)S(1)}, bf16[128,1024]{1,0:T(8,128)(2,1)}, u32[]{:S(2)}) copy-start(bf16[128,1024]{1,0:T(8,128)(2,1)} %param.21) | copy-start | bytes 786436
  6.5 90.1 %all-gather.3.cloned.1.call-start = ((), (), s32[]{:S(2)}) async-start(), calls=%async_computation.1 | async-start | bytes 18874368 | tf_op jit(solution)/shard_map/all_gather | solution.py:39
  7.3 304.2 %all-gather.5.cloned.1.call-start = ((), (), s32[]{:S(2)}) async-start(), calls=%async_computation.2 | async-start | bytes 35721216 | tf_op jit(solution)/shard_map/all_gather | solution.py:13
  112.2 2.4 copy-start.1
  112.2 2.6 copy-start.3
  113.7 383.5 %reduce-scatter.2.cloned.1.call-start = ((), (), s32[]{:S(2)}) async-start(), calls=%async_computation.3 | async-start | bytes 2359296 | tf_op jit(solution)/shard_map/reduce_scatter | solution.py:69
  421.5 45.3 %copy-start.2 = (f32[1024]{0:T(1024)S(1)}, f32[1024]{0:T(1024)}, u32[]{:S(2)}) copy-start(f32[1024]{0:T(1024)} %param.20) | copy-start | bytes 12292
Sparse Core Ops, SparseCore 0:
  9.0 87.5 all-gather.2
  113.8 197.6 all-gather.4
  464.2 32.9 reduce-scatter.1
where the time goes:
time: 509 us; the launch traced here: 507 us
  waiting for transfers between devices  315 us (62%)
  local copies, waits for them, and re-layouts  149 us (29%)
  matrix products  26.9 us (5%)
  between operations  13.9 us (3%)
    all_gather x1, waiting for transfers between devices, turned_gather(): filled, at, outs = (lax.all_gather(both, axis, axis=0, tiled=True), 0, [])  195 us
    all_gather x1, waiting for transfers between devices, on_device(): lax.all_gather(three_index, 'fit', axis=0, tiled=True)  88.6 us
    slice x3, local copies, waits for them, and re-layouts, turned_gather(): slab = filled[:, at:at + t[0].size].reshape(-1, *t.shape[1:])  65.4 us
    while x1, local copies, waits for them, and re-layouts, on_device(): partial_value = lax.fori_loop(0, block_count, advance, partial_value)  43.8 us
    reduce_scatter x1, waiting for transfers between devices, on_device(): lax.psum_scatter(partial_value.astype(jnp.bfloat16), 'fit', scatter_dimen...  30.3 us
    gather x8, local copies, waits for them, and re-layouts, advance(): left_rows = jnp.take(source, left_ids, axis=1)  15.7 us
    gather x8, local copies, waits for them, and re-layouts, advance(): right_rows = jnp.take(source, right_ids, axis=1)  15.7 us
    dot_general x1, matrix products, on_device(): jnp.dot(metric_factor, lax.all_gather(three_index, 'fit', axis=0, tiled=T...  13.6 us
  transfers between devices with their start and end apart: 3, of which 3 were waited for; matrix products, arithmetic and copies ran while one was open for 1% of the time, Pallas kernels for 0%

commit v1 on v0

--- a/solution.py
+++ b/solution.py
@@ -10,7 +10,13 @@
 def turned_gather(arrays, axis, dims):
     turned = [jnp.moveaxis(a, dim, 0) for a, dim in zip(arrays, dims)]
     both = jnp.concatenate([t.reshape(len(t), -1) for t in turned], axis=1)
-    filled, at, outs = (lax.all_gather(both, axis, axis=0, tiled=True), 0, [])
+    filled, at, outs = (
+        jnp.concatenate(
+            lax.all_to_all(jnp.stack([both] * lax.axis_size(axis)), axis, 0, 0), axis=0
+        ),
+        0,
+        [],
+    )
     for t, dim in zip(turned, dims):
         slab = filled[:, at : at + t[0].size].reshape(-1, *t.shape[1:])
         outs.append(jnp.moveaxis(slab, 0, dim))

time: 509 us -> 953 us (1.87)
  waiting for transfers between devices: 315 us -> 740 us
  local copies, waits for them, and re-layouts: 149 us -> 161 us
    all_to_all x0 -> x1, waiting for transfers between devices: none -> 623 us  [turned_gather(): lax.all_to_all(jnp.stack([both] * lax.axis_size(axis)), axis, 0, 0)]
    all_gather x1 -> x0, waiting for transfers between devices: 195 us -> none  [turned_gather(): filled, at, outs = (lax.all_gather(both, axis, axis=0, tiled=True), 0, [])]
    another operation x0 -> x1, local copies, waits for them, and re-layouts: none -> 11 us  [turned_gather(): jnp.stack([both] * lax.axis_size(axis))]
where the time goes in v1:
time: 953 us; the launch traced here: 950 us
  waiting for transfers between devices  740 us (78%)
  local copies, waits for them, and re-layouts  161 us (17%)
  matrix products  26.9 us (3%)
  between operations  14.2 us (1%)
    all_to_all x1, waiting for transfers between devices, turned_gather(): lax.all_to_all(jnp.stack([both] * lax.axis_size(axis)), axis, 0, 0)  623 us
    all_gather x1, waiting for transfers between devices, on_device(): lax.all_gather(three_index, 'fit', axis=0, tiled=True)  88.7 us
    slice x3, local copies, waits for them, and re-layouts, turned_gather(): slab = filled[:, at:at + t[0].size].reshape(-1, *t.shape[1:])  67.7 us
    while x1, local copies, waits for them, and re-layouts, on_device(): partial_value = lax.fori_loop(0, block_count, advance, partial_value)  43.1 us
    reduce_scatter x1, waiting for transfers between devices, on_device(): lax.psum_scatter(partial_value.astype(jnp.bfloat16), 'fit', scatter_dimen...  27 us
  transfers between devices with their start and end apart: 3, of which 3 were waited for; matrix products, arithmetic and copies ran while one was open for 1% of the time, Pallas kernels for 0%

profile of v1, /device:TPU:0, one launch (start us, length us, event | category | flops | bytes accessed | tf_op | source)
XLA Modules:
  0.0 950.3 jit_solution(11009331376860748284)
XLA Ops:
  8.0 88.7 %all-gather.2.cloned.1.call-done = bf16[4096,2048]{1,0:T(8,128)(2,1)} async-done(((bf16[512,2048]{1,0:T(8,128)(2,1)}), bf16[4096,2048]{1,0:T(8,128)(2,1)}) %all-gather.2.cloned.1.call-update) | async-done | bytes 16777232 | tf_op jit(solution)/shard_map/all_gather | solution.py:45
  96.7 13.6 %fusion.9 = bf16[64,16,8,128]{3,2,1,0:T(8,128)(2,1)S(1)} fusion(bf16[512,4096]{1,0:T(8,128)(2,1)} %param.14, bf16[4096,2048]{1,0:T(8,128)(2,1)} %all-gather.2.cloned.1.call-done), kind=kOutput, calls=%fused_computation.26 | convolution fusion | flops 8590983168 | bytes 23068672 | tf_op jit(solution)/shard_map/dot_general | solution.py:43
  112.3 11.0 %stack.2 = bf16[16,16,65537]{2,1,0:T(8,128)(2,1)} broadcast(bf16[16,65537]{1,0:T(8,128)(2,1)S(1)} %pad_maximum_fusion), dimensions={1,2} | broadcast | bytes 35652128 | tf_op jit(solution)/shard_map/stack | solution.py:15
  123.4 7.0 all-to-all-start
  133.0 623.4 %all-to-all-done = bf16[16,16,65537]{2,1,0:T(8,128)(2,1)} async-done(((bf16[16,16,65537]{2,1,0:T(8,128)(2,1)}), bf16[16,16,65537]{2,1,0:T(8,128)(2,1)}, u32[]{:S(2)}, u32[]{:S(2)}) %all-to-all-start) | async-done | bytes 33554976 | tf_op jit(solution)/shard_map/all_to_all | solution.py:15
  756.4 22.8 %slice.26 = bf16[256,65536]{1,0:T(8,128)(2,1)} slice(bf16[256,65537]{1,0:T(8,128)(2,1)} %bitcast.8), slice={[0:256], [0:65536]} | slice | bytes 67108864 | tf_op jit(solution)/shard_map/slice | solution.py:21
  779.2 43.9 %copy.23 = bf16[256,65536]{0,1:T(8,128)(2,1)} copy(bf16[256,65536]{1,0:T(8,128)(2,1)} %slice.26) | data formatting | bytes 67108864 | tf_op jit(solution)/shard_map/slice | solution.py:21
  823.1 43.1 %copy.24 = bf16[512,256,128]{2,0,1:T(8,128)(2,1)} copy(bf16[512,256,128]{1,2,0:T(8,128)(2,1)} %bitcast.42) | data formatting | bytes 67108864 | tf_op jit(solution)/shard_map/while | solution.py:72
  868.1 42.6 %while.10 = (s32[]{:T(128)}, bf16[64,128,128]{2,1,0:T(8,128)(2,1)}, s32[]{:T(128)}, s32[64]{0:T(128)S(1)}, bf16[512,256,128]{2,0,1:T(8,128)(2,1)}, /*index=5*/s3...) while((s32[]{:T(128)}, bf16[64,128,128]{2,1,0:T(8,128)(2,1)}, s32[]{:T(128)}, s32[64]{0:T(128)S(1)}, ...), condition=%wide.region_1.3_spmd, body=%wide.region_0.0_spmd.sunk | while | flops 135399520 | bytes 6824387 | solution.py:72
  868.2 2.0 gather_fusion
  870.2 2.0 gather_fusion.1
  873.5 2.0 gather_fusion
  875.5 2.0 gather_fusion.1
  878.8 2.0 gather_fusion
  880.8 2.0 gather_fusion.1
  884.1 2.0 gather_fusion
  886.1 2.0 gather_fusion.1
  889.5 2.0 gather_fusion
  891.4 2.0 gather_fusion.1
  894.8 2.0 gather_fusion
  896.8 2.0 gather_fusion.1
  900.1 2.0 gather_fusion
  913.4 27.0 %reduce-scatter.2.cloned.1.call-done = bf16[8,128,128]{2,1,0:T(8,128)(2,1)} async-done(((bf16[64,128,128]{2,1,0:T(8,128)(2,1)}), bf16[8,128,128]{2,1,0:T(8,128)(2,1)}) %reduce-scatter.2.cloned.1.call-update) | async-done | bytes 262160 | tf_op jit(solution)/shard_map/reduce_scatter | solution.py:75
  940.5 3.0 fusion.10
  (75 shorter events, 26.9 us)
Async XLA Ops:
  6.5 934.0 %copy-start = (bf16[128,1024]{1,0:T(8,128)(2,1)S(1)}, bf16[128,1024]{1,0:T(8,128)(2,1)}, u32[]{:S(2)}) copy-start(bf16[128,1024]{1,0:T(8,128)(2,1)} %param.21) | copy-start | bytes 786436
  6.5 90.1 %all-gather.2.cloned.1.call-start = ((), (), s32[]{:S(2)}) async-start(), calls=%async_computation.2 | async-start | bytes 18874368 | tf_op jit(solution)/shard_map/all_gather | solution.py:45
  123.3 7.2 copy-start.1
  123.3 7.4 copy-start.3
  123.4 633.0 %all-to-all-start = ((bf16[16,16,65537]{2,1,0:T(8,128)(2,1)}), bf16[16,16,65537]{2,1,0:T(8,128)(2,1)}, u32[]{:S(2)}, u32[]{:S(2)}) async-start(bf16[16,16,65537]{2,1,0:T(8,128)(2,1)} %stack.2), calls=%async_computation | async-start | bytes 67239936 | tf_op jit(solution)/shard_map/all_to_all | solution.py:15
  130.3 810.1 %reduce-scatter.2.cloned.1.call-start = ((), (), s32[]{:S(2)}) async-start(), calls=%async_computation.3 | async-start | bytes 2359296 | tf_op jit(solution)/shard_map/reduce_scatter | solution.py:75
  868.1 45.3 %copy-start.2 = (f32[1024]{0:T(1024)S(1)}, f32[1024]{0:T(1024)}, u32[]{:S(2)}) copy-start(f32[1024]{0:T(1024)} %param.20) | copy-start | bytes 12292
Sparse Core Ops, SparseCore 0:
  9.0 87.5 all-gather.1
  910.8 29.6 reduce-scatter.1
